TPU v7x, 32 devices: a whole 2x2x4 slice. The times are simulated.
32 devices in a mesh: batch: 2 (over x), row: 4 (over z), col: 4 (over y, core).
Axes of the slice: x: 2, y: 2, z: 4, core: 2. Of those that a mesh axis runs over, the one named last changes fastest.
Arguments:
- data_mat: bfloat16 [262144, 2048], P(('batch', 'row', 'col')), parts along dimension 0
- start_block: float32 [4096, 128], P('batch'), parts along dimension 0
Outputs:
- output 1: float32 [4096, 128], P('batch'), parts along dimension 0
- output 2: float32 [256], P('batch'), parts along dimension 0
There are 2 independent parts. A program takes and returns all parts, laid end to end along the dimension named above; each array names one.
All inputs are finite; a program needn't handle non-finite values.
Results may differ from a plain program's by a relative error of at most 0.001.
Values are sent between devices in bfloat16 or wider.
A program may use at most 1 GiB of HBM per device.

v0:
```python
import jax
import jax.numpy as jnp
from jax import lax
from jax.sharding import PartitionSpec as P

SWEEPS = 4
GROUP_AXES = ("row", "col")
ROW_CONTRACT = (((0,), (0,)), ((), ()))


def cholesky_qr2(z_rows):
    z_low = z_rows.astype(jnp.bfloat16)
    gram_one = lax.psum(lax.dot_general(z_low, z_low, ROW_CONTRACT, preferred_element_type=jnp.float32), GROUP_AXES)
    half_done = lax.linalg.triangular_solve(jnp.linalg.cholesky(gram_one), z_rows, left_side=False, lower=True, transpose_a=True)
    gram_two = lax.psum(lax.dot_general(half_done, half_done, ROW_CONTRACT, precision=lax.Precision.HIGHEST, preferred_element_type=jnp.float32), GROUP_AXES)
    return lax.linalg.triangular_solve(jnp.linalg.cholesky(gram_two), half_done, left_side=False, lower=True, transpose_a=True)


def solution(mesh):
    def device_sweeps(data_local, start_block):
        basis_low = start_block.astype(jnp.bfloat16)
        for sweep_idx in range(SWEEPS):
            projected = jnp.dot(data_local, basis_low, preferred_element_type=jnp.float32).astype(jnp.bfloat16)
            pulled_part = lax.dot_general(data_local, projected, ROW_CONTRACT, preferred_element_type=jnp.float32)
            pulled_rows = lax.psum_scatter(pulled_part, GROUP_AXES, scatter_dimension=0, tiled=True)
            q_rows = cholesky_qr2(pulled_rows)
            if sweep_idx < SWEEPS - 1:
                basis_low = lax.all_gather(q_rows.astype(jnp.bfloat16), GROUP_AXES, axis=0, tiled=True)
        q_basis = lax.all_gather(q_rows, GROUP_AXES, axis=0, tiled=True)
        final_proj = jnp.dot(data_local, q_basis.astype(jnp.bfloat16), preferred_element_type=jnp.float32)
        ritz_vals = lax.psum(jnp.sum(final_proj * final_proj, axis=0), GROUP_AXES)
        return q_basis, ritz_vals

    return jax.shard_map(device_sweeps, mesh=mesh, in_specs=(P(("batch", "row", "col"), None), P("batch", None)), out_specs=(P("batch", None), P("batch")), check_vma=False)
```

profile of v0, /device:TPU:0, one launch (start us, length us, event | category | flops | bytes accessed | tf_op | source)
XLA Modules:
  0.0 1457.4 jit_solution(16686786891727146503)
XLA Ops:
  7.2 35.9 %convolution_bitcast_fusion = f32[2048,128]{0,1:T(8,128)} fusion(bf16[8192,2048]{1,0:T(8,128)(2,1)} %param.5, f32[2048,128]{1,0:T(8,128)} %param.6), kind=kOutput, calls=%fused_computation.11 | convolution fusion | flops 8591245312 | bytes 35651584 | tf_op jit(solution)/shard_map/dot_general | solution.py:24
  43.2 60.3 %reduce-scatter.5.cloned.1.call-done = f32[128,128]{0,1:T(8,128)} async-done(((f32[2048,128]{0,1:T(8,128)}), f32[128,128]{0,1:T(8,128)}) %reduce-scatter.5.cloned.1.call-update) | async-done | bytes 65552 | tf_op jit(solution)/shard_map/reduce_scatter | solution.py:25
  103.5 1.7 fusion.57
  105.6 90.8 %all-reduce.9.cloned.1.call-done = f32[128,128]{0,1:T(8,128)} async-done(((f32[128,128]{0,1:T(8,128)}), f32[128,128]{0,1:T(8,128)}) %all-reduce.9.cloned.1.call-update) | async-done | bytes 65552 | tf_op jit(solution)/shard_map/psum | solution.py:13
  196.4 0.9 copy.5
  198.1 11.7 cholesky.134
  211.2 9.8 custom-call.12
  221.0 1.1 convolution_bitcast_fusion.8
  222.1 0.9 fusion.59
  223.6 88.4 %all-reduce.11.cloned.1.call-done = f32[128,128]{0,1:T(8,128)} async-done(((f32[128,128]{0,1:T(8,128)}), f32[128,128]{0,1:T(8,128)}) %all-reduce.11.cloned.1.call-update) | async-done | bytes 65552 | tf_op jit(solution)/shard_map/psum | solution.py:15
  312.0 0.9 copy.7
  313.8 11.7 cholesky.145
  326.9 9.8 custom-call.13
  337.0 20.9 %all_gather.12 = bf16[2048,128]{0,1:T(8,128)(2,1)S(1)} all-gather(bf16[128,128]{0,1:T(8,128)(2,1)S(1)} %fusion.7), channel_id=1, replica_groups=mesh['batch'=2,'row'=4,'col'=4] {'row','col'}, dimensions={0}, use_global_device_ids=true | all-gather | bytes 557056 | tf_op jit(solution)/shard_map/all_gather | solution.py:28
  357.9 31.7 %fusion.5 = f32[2048,128]{0,1:T(8,128)} fusion(bf16[8192,2048]{1,0:T(8,128)(2,1)} %param.5, bf16[2048,128]{0,1:T(8,128)(2,1)S(1)} %all_gather.12), kind=kOutput, calls=%fused_computation.10 | convolution fusion | flops 8590983168 | bytes 35127296 | tf_op jit(solution)/shard_map/dot_general | solution.py:24
  389.7 54.9 %reduce-scatter.7.cloned.1.call-done = f32[128,128]{0,1:T(8,128)} async-done(((f32[2048,128]{0,1:T(8,128)}), f32[128,128]{0,1:T(8,128)}) %reduce-scatter.7.cloned.1.call-update) | async-done | bytes 65552 | tf_op jit(solution)/shard_map/reduce_scatter | solution.py:25
  444.5 1.7 fusion.55
  446.5 90.8 %all-reduce.13.cloned.1.call-done = f32[128,128]{0,1:T(8,128)} async-done(((f32[128,128]{0,1:T(8,128)}), f32[128,128]{0,1:T(8,128)}) %all-reduce.13.cloned.1.call-update) | async-done | bytes 65552 | tf_op jit(solution)/shard_map/psum | solution.py:13
  537.2 0.9 copy.9
  538.2 0.9 fusion.32
  539.0 11.7 cholesky.156
  552.1 9.8 custom-call.14
  561.9 1.1 convolution_bitcast_fusion.6
  563.0 0.9 fusion.60
  564.2 88.7 %all-reduce.15.cloned.1.call-done = f32[128,128]{0,1:T(8,128)} async-done(((f32[128,128]{0,1:T(8,128)}), f32[128,128]{0,1:T(8,128)}) %all-reduce.15.cloned.1.call-update) | async-done | bytes 65552 | tf_op jit(solution)/shard_map/psum | solution.py:15
  652.9 0.9 copy.11
  654.7 11.7 cholesky.167
  667.8 9.8 custom-call.15
  677.9 20.9 %all_gather.13 = bf16[2048,128]{0,1:T(8,128)(2,1)S(1)} all-gather(bf16[128,128]{0,1:T(8,128)(2,1)S(1)} %fusion.8), channel_id=1, replica_groups=mesh['batch'=2,'row'=4,'col'=4] {'row','col'}, dimensions={0}, use_global_device_ids=true | all-gather | bytes 557056 | tf_op jit(solution)/shard_map/all_gather | solution.py:28
  698.8 31.6 %fusion.4 = f32[2048,128]{0,1:T(8,128)} fusion(bf16[8192,2048]{1,0:T(8,128)(2,1)} %param.5, bf16[2048,128]{0,1:T(8,128)(2,1)S(1)} %all_gather.13), kind=kOutput, calls=%fused_computation.9 | convolution fusion | flops 8590983168 | bytes 35127296 | tf_op jit(solution)/shard_map/dot_general | solution.py:24
  730.5 54.8 %reduce-scatter.9.cloned.1.call-done = f32[128,128]{0,1:T(8,128)} async-done(((f32[2048,128]{0,1:T(8,128)}), f32[128,128]{0,1:T(8,128)}) %reduce-scatter.9.cloned.1.call-update) | async-done | bytes 65552 | tf_op jit(solution)/shard_map/reduce_scatter | solution.py:25
  785.4 1.7 fusion.53
  787.4 90.8 %all-reduce.17.cloned.1.call-done = f32[128,128]{0,1:T(8,128)} async-done(((f32[128,128]{0,1:T(8,128)}), f32[128,128]{0,1:T(8,128)}) %all-reduce.17.cloned.1.call-update) | async-done | bytes 65552 | tf_op jit(solution)/shard_map/psum | solution.py:13
  878.2 0.9 copy.13
  879.1 0.9 fusion.28
  880.0 11.7 cholesky.178
  893.0 9.8 custom-call.16
  902.9 1.1 convolution_bitcast_fusion.4
  904.0 0.9 fusion.61
  905.4 88.5 %all-reduce.19.cloned.1.call-done = f32[128,128]{0,1:T(8,128)} async-done(((f32[128,128]{0,1:T(8,128)}), f32[128,128]{0,1:T(8,128)}) %all-reduce.19.cloned.1.call-update) | async-done | bytes 65552 | tf_op jit(solution)/shard_map/psum | solution.py:15
  993.9 0.9 copy.15
  995.7 11.7 cholesky.189
  1008.7 9.8 custom-call.17
  1018.8 20.9 %all_gather.14 = bf16[2048,128]{0,1:T(8,128)(2,1)S(1)} all-gather(bf16[128,128]{0,1:T(8,128)(2,1)S(1)} %fusion.9), channel_id=1, replica_groups=mesh['batch'=2,'row'=4,'col'=4] {'row','col'}, dimensions={0}, use_global_device_ids=true | all-gather | bytes 557056 | tf_op jit(solution)/shard_map/all_gather | solution.py:28
  1039.8 31.7 %fusion.3 = f32[2048,128]{0,1:T(8,128)} fusion(bf16[8192,2048]{1,0:T(8,128)(2,1)} %param.5, bf16[2048,128]{0,1:T(8,128)(2,1)S(1)} %all_gather.14), kind=kOutput, calls=%fused_computation.8 | convolution fusion | flops 8590983168 | bytes 35127296 | tf_op jit(solution)/shard_map/dot_general | solution.py:24
  1071.5 54.9 %reduce-scatter.11.cloned.1.call-done = f32[128,128]{0,1:T(8,128)} async-done(((f32[2048,128]{0,1:T(8,128)}), f32[128,128]{0,1:T(8,128)}) %reduce-scatter.11.cloned.1.call-update) | async-done | bytes 65552 | tf_op jit(solution)/shard_map/reduce_scatter | solution.py:25
  1126.4 1.7 fusion.51
  1128.3 90.9 %all-reduce.21.cloned.1.call-done = f32[128,128]{0,1:T(8,128)} async-done(((f32[128,128]{0,1:T(8,128)}), f32[128,128]{0,1:T(8,128)}) %all-reduce.21.cloned.1.call-update) | async-done | bytes 65552 | tf_op jit(solution)/shard_map/psum | solution.py:13
  1219.2 0.9 copy.17
  1220.1 0.9 fusion.24
  1221.0 11.7 cholesky.200
  1234.0 9.8 custom-call.18
  1243.8 1.1 convolution_bitcast_fusion.2
  1245.0 0.9 fusion.62
  1246.2 88.7 %all-reduce.23.cloned.1.call-done = f32[128,128]{0,1:T(8,128)} async-done(((f32[128,128]{0,1:T(8,128)}), f32[128,128]{0,1:T(8,128)}) %all-reduce.23.cloned.1.call-update) | async-done | bytes 65552 | tf_op jit(solution)/shard_map/psum | solution.py:15
  1334.9 0.9 copy.19
  1335.8 0.9 fusion.22
  1336.6 11.7 cholesky.211
  1349.7 9.8 custom-call.19
  1359.5 0.9 convolution_bitcast_fusion.1
  1360.5 35.9 %all-gather.2.cloned.1.call-done = f32[2048,128]{0,1:T(8,128)} async-done(((f32[128,128]{0,1:T(8,128)}), f32[2048,128]{0,1:T(8,128)}) %all-gather.2.cloned.1.call-update) | async-done | bytes 1048592 | tf_op jit(solution)/shard_map/all_gather | solution.py:29
  1396.3 19.6 %fusion.6 = f32[128]{0:T(128)S(1)} fusion(bf16[8192,2048]{1,0:T(8,128)(2,1)} %param.5, f32[2048,128]{0,1:T(8,128)} %all-gather.2.cloned.1.call-done), kind=kOutput, calls=%fused_computation.12 | convolution fusion | flops 4297326592 | bytes 34603520 | tf_op jit(solution)/shard_map/dot_general | solution.py:30
  1416.0 33.4 %psum.71 = f32[128]{0:T(128)} all-reduce(f32[128]{0:T(128)S(1)} %fusion.6), channel_id=1, replica_groups=mesh['batch'=2,'row'=4,'col'=4] {'row','col'}, use_global_device_ids=true, to_apply=%region_15.18 | all-reduce | flops 128 | bytes 1024 | tf_op jit(solution)/shard_map/psum | solution.py:31
  1449.4 1.3 copy.20
  (59 shorter events, 18.0 us)
Async XLA Ops:
  7.2 96.4 %reduce-scatter.5.cloned.1.call-start = ((), (), s32[]{:S(2)}) async-start(), calls=%async_computation.4 | async-start | bytes 1114112 | tf_op jit(solution)/shard_map/reduce_scatter | solution.py:25
  43.2 153.2 %all-reduce.9.cloned.1.call-start = ((), (), s32[]{:S(2)}) async-start(), calls=%async_computation.5 | async-start | bytes 131072 | tf_op jit(solution)/shard_map/psum | solution.py:13
  105.2 206.8 %all-reduce.11.cloned.1.call-start = ((), (), s32[]{:S(2)}) async-start(), calls=%async_computation.6 | async-start | bytes 131072 | tf_op jit(solution)/shard_map/psum | solution.py:15
  223.1 221.5 %reduce-scatter.7.cloned.1.call-start = ((), (), s32[]{:S(2)}) async-start(), calls=%async_computation.7 | async-start | bytes 1114112 | tf_op jit(solution)/shard_map/reduce_scatter | solution.py:25
  389.6 147.6 %all-reduce.13.cloned.1.call-start = ((), (), s32[]{:S(2)}) async-start(), calls=%async_computation.8 | async-start | bytes 131072 | tf_op jit(solution)/shard_map/psum | solution.py:13
  446.3 206.7 %all-reduce.15.cloned.1.call-start = ((), (), s32[]{:S(2)}) async-start(), calls=%async_computation.9 | async-start | bytes 131072 | tf_op jit(solution)/shard_map/psum | solution.py:15
  563.9 221.4 %reduce-scatter.9.cloned.1.call-start = ((), (), s32[]{:S(2)}) async-start(), calls=%async_computation.10 | async-start | bytes 1114112 | tf_op jit(solution)/shard_map/reduce_scatter | solution.py:25
  730.5 147.7 %all-reduce.17.cloned.1.call-start = ((), (), s32[]{:S(2)}) async-start(), calls=%async_computation.11 | async-start | bytes 131072 | tf_op jit(solution)/shard_map/psum | solution.py:13
  787.1 206.8 %all-reduce.19.cloned.1.call-start = ((), (), s32[]{:S(2)}) async-start(), calls=%async_computation.12 | async-start | bytes 131072 | tf_op jit(solution)/shard_map/psum | solution.py:15
  904.9 221.5 %reduce-scatter.11.cloned.1.call-start = ((), (), s32[]{:S(2)}) async-start(), calls=%async_computation.13 | async-start | bytes 1114112 | tf_op jit(solution)/shard_map/reduce_scatter | solution.py:25
  1071.5 147.7 %all-reduce.21.cloned.1.call-start = ((), (), s32[]{:S(2)}) async-start(), calls=%async_computation.14 | async-start | bytes 131072 | tf_op jit(solution)/shard_map/psum | solution.py:13
  1128.1 206.7 %all-reduce.23.cloned.1.call-start = ((), (), s32[]{:S(2)}) async-start(), calls=%async_computation.15 | async-start | bytes 131072 | tf_op jit(solution)/shard_map/psum | solution.py:15
  1245.9 150.4 %all-gather.2.cloned.1.call-start = ((), (), s32[]{:S(2)}) async-start(), calls=%async_computation.16 | async-start | bytes 1114112 | tf_op jit(solution)/shard_map/all_gather | solution.py:29
  1396.3 53.0 %copy-start = (f32[2048,128]{0,1:T(8,128)S(1)}, f32[2048,128]{0,1:T(8,128)}, u32[]{:S(2)}) copy-start(f32[2048,128]{0,1:T(8,128)} %all-gather.2.cloned.1.call-done) | copy-start | bytes 3145732
Sparse Core Ops, SparseCore 0:
  43.3 60.1 reduce-scatter.4
  107.6 88.7 all-reduce.8
  223.2 88.8 all-reduce.10
  389.7 54.7 reduce-scatter.6
  448.4 88.7 all-reduce.12
  564.1 88.8 all-reduce.14
  730.6 54.6 reduce-scatter.8
  789.4 88.7 all-reduce.16
  905.0 88.8 all-reduce.18
  1071.6 54.7 reduce-scatter.10
  1130.4 88.7 all-reduce.20
  1246.0 88.7 all-reduce.22
  1360.6 35.7 all-gather.1
where the time goes:
time: 1460 us
  waiting for transfers between devices  978 us (67%)
  other arithmetic  190 us (13%)
  matrix products  167 us (11%)
  blocking collectives  96.2 us (7%)
    psum x4, waiting for transfers between devices, cholesky_qr2(): lax.psum(lax.dot_general(z_low, z_low, ROW_CONTRACT, preferred_element_ty...  363 us
    psum x4, waiting for transfers between devices, cholesky_qr2(): lax.psum(lax.dot_general(half_done, half_done, ROW_CONTRACT, precision=la...  354 us
    reduce_scatter x4, waiting for transfers between devices, device_sweeps(): lax.psum_scatter(pulled_part, GROUP_AXES, scatter_dimension=0, tiled=True)  225 us
    dot_general x4, matrix products, device_sweeps(): lax.dot_general(data_local, projected, ROW_CONTRACT, preferred_element_ty...  131 us
    all_gather x3, blocking collectives, device_sweeps(): lax.all_gather(q_rows.astype(jnp.bfloat16), GROUP_AXES, axis=0, tiled=True)  62.8 us
    another operation x12, other arithmetic, cholesky_qr2(): jnp.linalg.cholesky(gram_one)  49.6 us
    another operation x12, other arithmetic, cholesky_qr2(): jnp.linalg.cholesky(gram_two)  49.6 us
    another operation x8, other arithmetic, cholesky_qr2(): lax.linalg.triangular_solve(jnp.linalg.cholesky(gram_two), half_done, lef...  41.9 us
  transfers between devices with their start and end apart: 13, of which 13 were waited for; matrix products, arithmetic and copies ran while one was open for 0% of the time, Pallas kernels for 0%

commit v1 on v0

v1 whole, which is shorter than its diff:
```python
import functools

import jax
import jax.numpy as jnp
from jax import lax
from jax.experimental import pallas as pl
from jax.experimental.pallas import tpu as pltpu
from jax.sharding import PartitionSpec as P

SWEEPS = 4
NB = 32
HI = lax.Precision.HIGHEST
NT = (((1,), (1,)), ((), ()))
TN = (((0,), (0,)), ((), ()))
F32 = jnp.float32
BF16 = jnp.bfloat16


def split3(v):
    hi = v.astype(BF16)
    rest = v - hi.astype(F32)
    mid = rest.astype(BF16)
    low = (rest - mid.astype(F32)).astype(BF16)
    return hi, mid, low


def inverse_factor(gram):
    n = gram.shape[0]
    groups = NB // 8
    sub = lax.broadcasted_iota(jnp.int32, (8, n), 0)
    lane = lax.broadcasted_iota(jnp.int32, (8, n), 1)
    m_rows = [gram[8 * g : 8 * g + 8, :] for g in range(n // 8)]
    n_rows = [jnp.where(lane == sub + 8 * g, 1.0, 0.0).astype(F32) for g in range(n // 8)]
    out = []
    for blk in range(n // NB):
        g0 = blk * groups
        mp = m_rows[g0 : g0 + groups]
        np_ = n_rows[g0 : g0 + groups]
        cols = [
            [None if g < i // 8 else jnp.broadcast_to(mp[g][:, blk * NB + i : blk * NB + i + 1], (8, n)) for g in range(groups)]
            for i in range(NB)
        ]
        piv = [jnp.ones((8, n), F32) for _ in range(groups)]
        for j in range(NB):
            gj, sj = j // 8, j % 8
            d_b = jnp.broadcast_to(cols[j][gj][sj : sj + 1, :], (8, n))
            piv[gj] = jnp.where(sub == sj, d_b, piv[gj])
            rinv = 1.0 / d_b
            mrow = jnp.broadcast_to(mp[gj][sj : sj + 1, :], (8, n))
            nrow = jnp.broadcast_to(np_[gj][sj : sj + 1, :], (8, n))
            mult = [None] * groups
            for g in range(gj, groups):
                if g == gj and sj == 7:
                    continue
                c = cols[j][g] * rinv
                mult[g] = jnp.where(sub > sj, c, 0.0) if g == gj else c
            for i in range(j + 1, NB):
                u = jnp.broadcast_to(cols[j][i // 8][i % 8 : i % 8 + 1, :], (8, n))
                for g in range(i // 8, groups):
                    cols[i][g] = cols[i][g] - mult[g] * u
            for g in range(gj, groups):
                if mult[g] is not None:
                    mp[g] = mp[g] - mult[g] * mrow
                    np_[g] = np_[g] - mult[g] * nrow
        for g in range(groups):
            out.append(np_[g] * lax.rsqrt(piv[g]))
        if blk + 1 < n // NB:
            m_pan = jnp.concatenate(mp, axis=0)
            n_pan = jnp.concatenate(np_, axis=0)
            scaled = m_pan * (1.0 / jnp.concatenate(piv, axis=0))
            lh, lm, ll = split3(scaled)
            both = jnp.concatenate([m_pan, n_pan], axis=1)
            rh, rm, rl = split3(both)
            left = jnp.concatenate([ll, lm, lh, lm, lh, lh], axis=0)
            right = jnp.concatenate([rh, rm, rl, rh, rm, rh], axis=0)
            upd = lax.dot_general(left, right, TN, preferred_element_type=F32)
            for g in range(g0 + groups, n // 8):
                m_rows[g] = m_rows[g] - upd[8 * g : 8 * g + 8, :n]
                n_rows[g] = n_rows[g] - upd[8 * g : 8 * g + 8, n:]
    return jnp.concatenate(out, axis=0)


def kernel(
    a_hbm, x0_ref, q_ref, r_ref,
    a_v, wt, xt, part, ra, sb, rb, sc, rc, zfull, zlow, ytr, rbuf,
    load_sem, as_, ar, bs, br, cs, cr, zs, zr, ys, yr, ks, kr, rs, rr,
):
    rows, feats = a_v.shape
    n_chunks = load_sem.shape[0]
    chunk = rows // n_chunks
    z = lax.axis_index("row")
    col = lax.axis_index("col")
    y = col // 2
    c = col % 2
    zh, zl = z // 2, z % 2

    def zflip(m):
        return 2 * ((zh + m // 2) % 2) + (zl + m % 2) % 2

    def fidx(core, yy, zz):
        return zz * 4 + yy * 2 + core

    peer_core = y * 2 + 1 - c
    peer_y = (1 - y) * 2 + c

    def rcopy(src, dst, ssem, rsem, row, column):
        return pltpu.make_async_remote_copy(
            src_ref=src, dst_ref=dst, send_sem=ssem, recv_sem=rsem,
            device_id={"row": row, "col": column}, device_id_type=pl.DeviceIdType.MESH,
        )

    def load(i):
        span = pl.ds(i * chunk, chunk)
        return pltpu.make_async_copy(a_hbm.at[span], a_v.at[span], load_sem.at[i])

    for i in range(n_chunks):
        load(i).start()

    barrier = pltpu.get_barrier_semaphore()
    for row, column in [(z, peer_core), (z, peer_y), (zflip(1), col), (zflip(2), col), (zflip(3), col)]:
        pl.semaphore_signal(barrier, inc=1, device_id={"row": row, "col": column}, device_id_type=pl.DeviceIdType.MESH)
    pl.semaphore_wait(barrier, 5)

    for i in range(feats // 256):
        span = pl.ds(i * 256, 256)
        xt[:, span] = x0_ref[span, :].T.astype(BF16)

    def send_core(s):
        return rcopy(part.at[s, 1 - c], ra.at[s], as_.at[s], ar.at[s], z, peer_core)

    def send_y(t):
        return rcopy(sb.at[t], rb.at[t], bs.at[t], br.at[t], z, peer_y)

    def send_z(k):
        return rcopy(sc.at[k], rc.at[k], cs.at[k], cr.at[k], zflip(3 - k), col)

    def gather_z(m):
        f = fidx(c, y, z)
        return rcopy(zfull.at[f], zfull.at[f], zs.at[m], zr.at[m], zflip(m), col)

    def gather_y(m):
        f = fidx(c, y, zflip(m))
        return rcopy(zfull.at[f], zfull.at[f], ys.at[m], yr.at[m], z, peer_y)

    def gather_core(m, yy):
        f = fidx(c, (y + yy) % 2, zflip(m))
        return rcopy(zfull.at[f], zfull.at[f], ks.at[yy * 4 + m], kr.at[yy * 4 + m], z, peer_core)

    def sweep(it, carry):
        def project(i, carry):
            @pl.when(it == 0)
            def _():
                load(i).wait()

            span = pl.ds(pl.multiple_of(i * chunk, chunk), chunk)
            got = lax.dot_general(xt[...], a_v[span, :], NT, preferred_element_type=F32)
            wt[:, span] = got.astype(BF16)
            return carry

        lax.fori_loop(0, n_chunks, project, 0)

        def pull(s, carry):
            m = 3 - s % 4
            base = fidx(0, (y + 1 + s // 4) % 2, zflip(m)) * 128
            acc = jnp.dot(wt[...], a_v[:, pl.ds(pl.multiple_of(base, 256), 256)], preferred_element_type=F32)
            part[s, 0] = acc[:, :128]
            part[s, 1] = acc[:, 128:]
            send_core(s).start()

            @pl.when((s >= 2) & (s < 6))
            def _():
                t = s - 2
                send_core(t).wait_recv()
                sb[t] = part[t, c] + ra[t]
                send_y(t).start()

            return carry

        lax.fori_loop(0, 8, pull, 0)

        for k in range(4):
            send_core(4 + k).wait_recv()
            send_y(k).wait_recv()
            total = (part[4 + k, c] + ra[4 + k]) + rb[k]
            sc[k] = total
            if k < 3:
                send_z(k).start()
        me = fidx(c, y, z)
        for k in range(3):
            send_z(2 - k).wait_recv()
            sc[3] = sc[3] + rc[2 - k]
        zfull[me] = sc[3]

        gather_y(0).start()
        for m in (1, 2, 3):
            gather_z(m).start()
        gather_core(0, 0).start()
        gather_y(0).wait_recv()
        gather_core(0, 1).start()
        for m in (1, 2, 3):
            gather_z(m).wait_recv()
            gather_y(m).start()
            gather_core(m, 0).start()
        for m in (1, 2, 3):
            gather_y(m).wait_recv()
            gather_core(m, 1).start()
        for yy in (0, 1):
            for m in range(4):
                gather_core(m, yy).wait_recv()

        for f in range(16):
            zlow[:, f * 128 : f * 128 + 128] = zfull[f].astype(BF16)
        low = zlow[...]
        inv = inverse_factor(lax.dot_general(low, low, NT, preferred_element_type=F32))
        for f in range(0, 16, 2):
            two = jnp.concatenate([zfull[f], zfull[f + 1]], axis=1)
            ytr[:, f * 128 : f * 128 + 256] = jnp.dot(inv, two, precision=HI, preferred_element_type=F32)
        half = ytr[...]
        inv = inverse_factor(lax.dot_general(half, half, NT, precision=HI, preferred_element_type=F32))
        for f in range(0, 16, 2):
            span = slice(f * 128, f * 128 + 256)
            new = jnp.dot(inv, ytr[:, span], precision=HI, preferred_element_type=F32)
            xt[:, span] = new.astype(BF16)
            ytr[:, span] = new

        for s in range(8):
            send_core(s).wait_send()
        for t in range(4):
            send_y(t).wait_send()
            gather_y(t).wait_send()
        for k in range(3):
            send_z(k).wait_send()
            gather_z(k + 1).wait_send()
        for yy in (0, 1):
            for m in range(4):
                gather_core(m, yy).wait_send()
        return carry

    lax.fori_loop(0, SWEEPS, sweep, 0)

    for i in range(feats // 256):
        span = slice(i * 256, i * 256 + 256)
        q_ref[span, :] = ytr[:, span].T

    def ritz(i, acc):
        span = pl.ds(pl.multiple_of(i * chunk, chunk), chunk)
        got = lax.dot_general(xt[...], a_v[span, :], NT, preferred_element_type=F32)
        for j in range(chunk // 128):
            piece = got[:, j * 128 : j * 128 + 128]
            acc = acc + piece * piece
        return acc

    acc = lax.fori_loop(0, n_chunks, ritz, jnp.zeros((128, 128), F32)).T
    rbuf[0] = jnp.sum(acc.reshape(16, 8, 128), axis=0)
    step = rcopy(rbuf.at[0], rbuf.at[1], rs.at[0], rr.at[0], z, peer_core)
    step.start()
    step.wait()
    rbuf[2] = rbuf[0] + rbuf[1]
    step = rcopy(rbuf.at[2], rbuf.at[3], rs.at[1], rr.at[1], z, peer_y)
    step.start()
    step.wait()
    rbuf[4 + z] = rbuf[2] + rbuf[3]
    sends = [rcopy(rbuf.at[4 + z], rbuf.at[4 + z], rs.at[1 + m], rr.at[1 + m], zflip(m), col) for m in (1, 2, 3)]
    for copy in sends:
        copy.start()
    for copy in sends:
        copy.wait()
    whole = (rbuf[4] + rbuf[5]) + (rbuf[6] + rbuf[7])
    r_ref[...] = jnp.sum(whole, axis=0, keepdims=True)


def solution(mesh):
    def local(data_local, start_block):
        rows, feats = data_local.shape
        n_chunks = max(1, rows // 1024)
        dma = pltpu.SemaphoreType.DMA
        block = (128, 128)
        q, r = pl.pallas_call(
            kernel,
            out_shape=(jax.ShapeDtypeStruct((feats, 128), F32), jax.ShapeDtypeStruct((1, 128), F32)),
            in_specs=[pl.BlockSpec(memory_space=pl.ANY), pl.BlockSpec(memory_space=pltpu.VMEM)],
            out_specs=(pl.BlockSpec(memory_space=pltpu.VMEM), pl.BlockSpec(memory_space=pltpu.VMEM)),
            scratch_shapes=[
                pltpu.VMEM((rows, feats), BF16),
                pltpu.VMEM((128, rows), BF16),
                pltpu.VMEM((128, feats), BF16),
                pltpu.VMEM((8, 2) + block, F32),
                pltpu.VMEM((8,) + block, F32),
                pltpu.VMEM((4,) + block, F32),
                pltpu.VMEM((4,) + block, F32),
                pltpu.VMEM((4,) + block, F32),
                pltpu.VMEM((3,) + block, F32),
                pltpu.VMEM((16,) + block, F32),
                pltpu.VMEM((128, feats), BF16),
                pltpu.VMEM((128, feats), F32),
                pltpu.VMEM((8, 8, 128), F32),
                dma((n_chunks,)),
                dma((8,)), dma((8,)),
                dma((4,)), dma((4,)),
                dma((3,)), dma((3,)),
                dma((4,)), dma((4,)),
                dma((4,)), dma((4,)),
                dma((8,)), dma((8,)),
                dma((5,)), dma((5,)),
            ],
            compiler_params=pltpu.CompilerParams(
                collective_id=0, has_side_effects=True, vmem_limit_bytes=60 * 1024 * 1024
            ),
            name="subspace",
        )(data_local, start_block)
        return q, r.reshape(128)

    return jax.shard_map(
        local, mesh=mesh, in_specs=(P(("batch", "row", "col"), None), P("batch", None)),
        out_specs=(P("batch", None), P("batch")), check_vma=False,
    )
```

time: 1460 us -> 224 us (0.15)
  waiting for transfers between devices: 978 us -> 0 us
  Pallas kernels: 0 us -> 220 us
  other arithmetic: 190 us -> 0 us
  matrix products: 167 us -> 0 us
  blocking collectives: 96.2 us -> 0 us
    psum x8 -> x0, waiting for transfers between devices: 717 us -> none  [the longest x4 363 us: cholesky_qr2(): lax.psum(lax.dot_general(z_low, z_low, ROW_CONTRACT, preferred_element_ty...]
    reduce_scatter x4 -> x0, waiting for transfers between devices: 225 us -> none  [device_sweeps(): lax.psum_scatter(pulled_part, GROUP_AXES, scatter_dimension=0, tiled=True)]
    pallas_call x0 -> x1, Pallas kernels: none -> 220 us  [local(): pl.pallas_call(kernel, out_shape=(jax.ShapeDtypeStruct((feats, 128), F32)...]
    another operation x40 -> x0, other arithmetic: 183 us -> none  [the longest x12 49.6 us: cholesky_qr2(): jnp.linalg.cholesky(gram_one)]
    dot_general x13 -> x0, matrix products: 161 us -> none  [the longest x4 131 us: device_sweeps(): lax.dot_general(data_local, projected, ROW_CONTRACT, preferred_element_ty...]
    all_gather x3 -> x0, blocking collectives: 62.8 us -> none  [device_sweeps(): lax.all_gather(q_rows.astype(jnp.bfloat16), GROUP_AXES, axis=0, tiled=True)]
    all_gather x1 -> x0, waiting for transfers between devices: 35.9 us -> none  [device_sweeps(): q_basis = lax.all_gather(q_rows, GROUP_AXES, axis=0, tiled=True)]
    psum x1 -> x0, blocking collectives: 33.4 us -> none  [device_sweeps(): ritz_vals = lax.psum(jnp.sum(final_proj * final_proj, axis=0), GROUP_AXES)]
  transfers between devices with their start and end apart: 13 -> 0, of which waited for: 13 -> 0; matrix products, arithmetic and copies ran while one was open for 0% -> 0% of each run, Pallas kernels for 0% -> 0%
where the time goes in v1:
time: 224 us
  Pallas kernels  220 us (98%)
  local copies, waits for them, and re-layouts  3.38 us (2%)
    pallas_call x1, Pallas kernels, local(): pl.pallas_call(kernel, out_shape=(jax.ShapeDtypeStruct((feats, 128), F32)...  220 us

profile of v1, /device:TPU:0, one launch (start us, length us, event | category | flops | bytes accessed | tf_op | source)
XLA Modules:
  0.0 223.8 jit_solution(12540191356923383073)
XLA Ops:
  0.6 219.7 %subspace.1 = (f32[2048,128]{1,0:T(8,128)}, f32[1,128]{1,0:T(1,128)}) custom-call(bf16[8192,2048]{1,0:T(8,128)(2,1)} %a_hbm.1, f32[2048,128]{1,0:T(8,128)} %x0_ref.1), custom_call_target="tpu_custom_call" | custom-call | tf_op jit(solution)/shard_map/subspace/pallas_call | solution.py:278
  220.4 2.3 %copy.6 = f32[2048,128]{1,0:T(8,128)} copy(f32[2048,128]{1,0:T(8,128)} %get-tuple-element.8) | data formatting | bytes 2097152
  222.6 1.1 copy.7

commit v2 on v1

--- a/solution.py
+++ b/solution.py
@@ -11,6 +11,7 @@
 NB = 32
 HI = lax.Precision.HIGHEST
 NT = (((1,), (1,)), ((), ()))
+PULLS = (((0,), ()), ((1, 2), (0,)), ((3, 4), (1, 2)), ((5, 6, 7), (3,)))
 TN = (((0,), (0,)), ((), ()))
 F32 = jnp.float32
 BF16 = jnp.bfloat16
@@ -80,10 +81,23 @@
     return jnp.concatenate(out, axis=0)
 
 
+def solve_pieces(inv):
+    hi, mid, low = split3(inv)
+    return jnp.concatenate([hi, mid], axis=1), jnp.concatenate([hi, low], axis=1)
+
+
+def apply_pieces(pieces, v):
+    hm, hl = pieces
+    vh, vm, vl = split3(v)
+    out = jnp.dot(hm, jnp.concatenate([vl, vm], axis=0), preferred_element_type=F32)
+    out = out + jnp.dot(hm, jnp.concatenate([vm, vh], axis=0), preferred_element_type=F32)
+    return out + jnp.dot(hl, jnp.concatenate([vh, vh], axis=0), preferred_element_type=F32)
+
+
 def kernel(
-    a_hbm, x0_ref, q_ref, r_ref,
-    a_v, wt, xt, part, ra, sb, rb, sc, rc, zfull, zlow, ytr, rbuf,
-    load_sem, as_, ar, bs, br, cs, cr, zs, zr, ys, yr, ks, kr, rs, rr,
+    a_hbm, x0_hbm, q_hbm, r_ref,
+    a_v, wt, xs, qx, part, ra, sb, rb, sc, rc, zfull, zlow, zmid, ylow, ytr, rbuf,
+    load_sem, io_sem, as_, ar, bs, br, cs, cr, zs, zr, ys, yr, ks, kr, rs, rr,
 ):
     rows, feats = a_v.shape
     n_chunks = load_sem.shape[0]
@@ -102,6 +116,7 @@
 
     peer_core = y * 2 + 1 - c
     peer_y = (1 - y) * 2 + c
+    peer_both = (1 - y) * 2 + 1 - c
 
     def rcopy(src, dst, ssem, rsem, row, column):
         return pltpu.make_async_remote_copy(
@@ -113,17 +128,17 @@
         span = pl.ds(i * chunk, chunk)
         return pltpu.make_async_copy(a_hbm.at[span], a_v.at[span], load_sem.at[i])
 
+    start = pltpu.make_async_copy(x0_hbm, qx, io_sem.at[0])
+    start.start()
     for i in range(n_chunks):
         load(i).start()
 
     barrier = pltpu.get_barrier_semaphore()
-    for row, column in [(z, peer_core), (z, peer_y), (zflip(1), col), (zflip(2), col), (zflip(3), col)]:
+    for row, column in [(z, peer_core), (z, peer_y), (z, peer_both), (zflip(1), col), (zflip(2), col), (zflip(3), col)]:
         pl.semaphore_signal(barrier, inc=1, device_id={"row": row, "col": column}, device_id_type=pl.DeviceIdType.MESH)
-    pl.semaphore_wait(barrier, 5)
-
-    for i in range(feats // 256):
-        span = pl.ds(i * 256, 256)
-        xt[:, span] = x0_ref[span, :].T.astype(BF16)
+
+    start.wait()
+    xs[...] = qx[...].astype(BF16)
 
     def send_core(s):
         return rcopy(part.at[s, 1 - c], ra.at[s], as_.at[s], ar.at[s], z, peer_core)
@@ -146,37 +161,30 @@
         f = fidx(c, (y + yy) % 2, zflip(m))
         return rcopy(zfull.at[f], zfull.at[f], ks.at[yy * 4 + m], kr.at[yy * 4 + m], z, peer_core)
 
+    def project_rows(first, count):
+        for k in range(count // chunk):
+            base = first + k * chunk
+            got = jnp.dot(a_v[pl.ds(pl.multiple_of(base, chunk), chunk), :], xs[...], preferred_element_type=F32)
+            for j in range(chunk // 128):
+                wt[:, pl.ds(pl.multiple_of(base + j * 128, 128), 128)] = got[j * 128 : j * 128 + 128].T.astype(BF16)
+
+    def pull(s):
+        m = 3 - s % 4
+        base = fidx(0, (y + 1 + s // 4) % 2, zflip(m)) * 128
+        return jnp.dot(wt[...], a_v[:, pl.ds(pl.multiple_of(base, 256), 256)], preferred_element_type=F32)
+
     def sweep(it, carry):
-        def project(i, carry):
-            @pl.when(it == 0)
-            def _():
-                load(i).wait()
-
-            span = pl.ds(pl.multiple_of(i * chunk, chunk), chunk)
-            got = lax.dot_general(xt[...], a_v[span, :], NT, preferred_element_type=F32)
-            wt[:, span] = got.astype(BF16)
-            return carry
-
-        lax.fori_loop(0, n_chunks, project, 0)
-
-        def pull(s, carry):
-            m = 3 - s % 4
-            base = fidx(0, (y + 1 + s // 4) % 2, zflip(m)) * 128
-            acc = jnp.dot(wt[...], a_v[:, pl.ds(pl.multiple_of(base, 256), 256)], preferred_element_type=F32)
-            part[s, 0] = acc[:, :128]
-            part[s, 1] = acc[:, 128:]
-            send_core(s).start()
-
-            @pl.when((s >= 2) & (s < 6))
-            def _():
-                t = s - 2
+        for group, ready in PULLS:
+            got = [pull(s) for s in group]
+            for s, acc in zip(group, got):
+                part[s, 0] = acc[:, :128]
+                part[s, 1] = acc[:, 128:]
+            for s in group:
+                send_core(s).start()
+            for t in ready:
                 send_core(t).wait_recv()
                 sb[t] = part[t, c] + ra[t]
                 send_y(t).start()
-
-            return carry
-
-        lax.fori_loop(0, 8, pull, 0)
 
         for k in range(4):
             send_core(4 + k).wait_recv()
@@ -212,16 +220,25 @@
             zlow[:, f * 128 : f * 128 + 128] = zfull[f].astype(BF16)
         low = zlow[...]
         inv = inverse_factor(lax.dot_general(low, low, NT, preferred_element_type=F32))
-        for f in range(0, 16, 2):
-            two = jnp.concatenate([zfull[f], zfull[f + 1]], axis=1)
-            ytr[:, f * 128 : f * 128 + 256] = jnp.dot(inv, two, precision=HI, preferred_element_type=F32)
-        half = ytr[...]
-        inv = inverse_factor(lax.dot_general(half, half, NT, precision=HI, preferred_element_type=F32))
+        pieces = solve_pieces(inv)
         for f in range(0, 16, 2):
             span = slice(f * 128, f * 128 + 256)
-            new = jnp.dot(inv, ytr[:, span], precision=HI, preferred_element_type=F32)
-            xt[:, span] = new.astype(BF16)
+            new = apply_pieces(pieces, jnp.concatenate([zfull[f], zfull[f + 1]], axis=1))
             ytr[:, span] = new
+            hi, mid, lo = split3(new)
+            zlow[:, span] = hi
+            zmid[:, span] = mid
+            ylow[:, span] = lo
+        hi, mid = zlow[...], zmid[...]
+        wide = lax.dot_general(hi, jnp.concatenate([hi, mid], axis=0), NT, preferred_element_type=F32)
+        cross = wide[:, 128:] + lax.dot_general(hi, ylow[...], NT, preferred_element_type=F32)
+        gram = (lax.dot_general(mid, mid, NT, preferred_element_type=F32) + (cross + cross.T)) + wide[:, :128]
+        pieces = solve_pieces(inverse_factor(gram))
+        for f in range(0, 16, 2):
+            span = slice(f * 128, f * 128 + 256)
+            new = apply_pieces(pieces, ytr[:, span]).T
+            xs[span, :] = new.astype(BF16)
+            qx[span, :] = new
 
         for s in range(8):
             send_core(s).wait_send()
@@ -234,39 +251,58 @@
         for yy in (0, 1):
             for m in range(4):
                 gather_core(m, yy).wait_send()
+
+        @pl.when(it < SWEEPS - 1)
+        def _():
+            body = min(rows, 4 * chunk)
+
+            def project(i, carry):
+                project_rows(i * body, body)
+                return carry
+
+            lax.fori_loop(0, rows // body, project, 0)
+
         return carry
 
+    def first_project(i, carry):
+        load(i).wait()
+        project_rows(i * chunk, chunk)
+        return carry
+
+    lax.fori_loop(0, n_chunks, first_project, 0)
+    pl.semaphore_wait(barrier, 6)
     lax.fori_loop(0, SWEEPS, sweep, 0)
 
-    for i in range(feats // 256):
-        span = slice(i * 256, i * 256 + 256)
-        q_ref[span, :] = ytr[:, span].T
+    finish = pltpu.make_async_copy(qx, q_hbm, io_sem.at[1])
+    finish.start()
+    body = min(rows, 2 * chunk)
 
     def ritz(i, acc):
-        span = pl.ds(pl.multiple_of(i * chunk, chunk), chunk)
-        got = lax.dot_general(xt[...], a_v[span, :], NT, preferred_element_type=F32)
-        for j in range(chunk // 128):
-            piece = got[:, j * 128 : j * 128 + 128]
-            acc = acc + piece * piece
+        for k in range(body // chunk):
+            span = pl.ds(pl.multiple_of(i * body + k * chunk, chunk), chunk)
+            got = jnp.dot(a_v[span, :], xs[...], preferred_element_type=F32)
+            acc = acc + jnp.sum((got * got).reshape(chunk // 64, 64, 128), axis=0)
         return acc
 
-    acc = lax.fori_loop(0, n_chunks, ritz, jnp.zeros((128, 128), F32)).T
-    rbuf[0] = jnp.sum(acc.reshape(16, 8, 128), axis=0)
-    step = rcopy(rbuf.at[0], rbuf.at[1], rs.at[0], rr.at[0], z, peer_core)
-    step.start()
-    step.wait()
-    rbuf[2] = rbuf[0] + rbuf[1]
-    step = rcopy(rbuf.at[2], rbuf.at[3], rs.at[1], rr.at[1], z, peer_y)
-    step.start()
-    step.wait()
-    rbuf[4 + z] = rbuf[2] + rbuf[3]
-    sends = [rcopy(rbuf.at[4 + z], rbuf.at[4 + z], rs.at[1 + m], rr.at[1 + m], zflip(m), col) for m in (1, 2, 3)]
+    acc = lax.fori_loop(0, rows // body, ritz, jnp.zeros((64, 128), F32))
+    rbuf[z] = jnp.sum(acc.reshape(8, 8, 128), axis=0)
+    sends = [rcopy(rbuf.at[z], rbuf.at[z], rs.at[m - 1], rr.at[m - 1], zflip(m), col) for m in (1, 2, 3)]
+    for copy in sends:
+        copy.start()
+    for copy in sends:
+        copy.wait()
+    rbuf[4 + col] = (rbuf[0] + rbuf[1]) + (rbuf[2] + rbuf[3])
+    sends = [
+        rcopy(rbuf.at[4 + col], rbuf.at[4 + col], rs.at[3 + i], rr.at[3 + i], z, column)
+        for i, column in enumerate((peer_core, peer_y, peer_both))
+    ]
     for copy in sends:
         copy.start()
     for copy in sends:
         copy.wait()
     whole = (rbuf[4] + rbuf[5]) + (rbuf[6] + rbuf[7])
     r_ref[...] = jnp.sum(whole, axis=0, keepdims=True)
+    finish.wait()
 
 
 def solution(mesh):
@@ -278,12 +314,13 @@
         q, r = pl.pallas_call(
             kernel,
             out_shape=(jax.ShapeDtypeStruct((feats, 128), F32), jax.ShapeDtypeStruct((1, 128), F32)),
-            in_specs=[pl.BlockSpec(memory_space=pl.ANY), pl.BlockSpec(memory_space=pltpu.VMEM)],
-            out_specs=(pl.BlockSpec(memory_space=pltpu.VMEM), pl.BlockSpec(memory_space=pltpu.VMEM)),
+            in_specs=[pl.BlockSpec(memory_space=pl.ANY), pl.BlockSpec(memory_space=pl.ANY)],
+            out_specs=(pl.BlockSpec(memory_space=pl.ANY), pl.BlockSpec(memory_space=pltpu.VMEM)),
             scratch_shapes=[
                 pltpu.VMEM((rows, feats), BF16),
                 pltpu.VMEM((128, rows), BF16),
-                pltpu.VMEM((128, feats), BF16),
+                pltpu.VMEM((feats, 128), BF16),
+                pltpu.VMEM((feats, 128), F32),
                 pltpu.VMEM((8, 2) + block, F32),
                 pltpu.VMEM((8,) + block, F32),
                 pltpu.VMEM((4,) + block, F32),
@@ -292,16 +329,18 @@
                 pltpu.VMEM((3,) + block, F32),
                 pltpu.VMEM((16,) + block, F32),
                 pltpu.VMEM((128, feats), BF16),
+                pltpu.VMEM((128, feats), BF16),
+                pltpu.VMEM((128, feats), BF16),
                 pltpu.VMEM((128, feats), F32),
                 pltpu.VMEM((8, 8, 128), F32),
-                dma((n_chunks,)),
+                dma((n_chunks,)), dma((2,)),
                 dma((8,)), dma((8,)),
                 dma((4,)), dma((4,)),
                 dma((3,)), dma((3,)),
                 dma((4,)), dma((4,)),
                 dma((4,)), dma((4,)),
                 dma((8,)), dma((8,)),
-                dma((5,)), dma((5,)),
+                dma((6,)), dma((6,)),
             ],
             compiler_params=pltpu.CompilerParams(
                 collective_id=0, has_side_effects=True, vmem_limit_bytes=60 * 1024 * 1024

time: 224 us -> 207 us (0.924)
  Pallas kernels: 220 us -> 203 us
    pallas_call x1, Pallas kernels: 220 us -> 203 us  [local(): pl.pallas_call(kernel, out_shape=(jax.ShapeDtypeStruct((feats, 128), F32)...]
where the time goes in v2:
time: 207 us
  Pallas kernels  203 us (98%)
  local copies, waits for them, and re-layouts  3.38 us (2%)
    pallas_call x1, Pallas kernels, local(): pl.pallas_call(kernel, out_shape=(jax.ShapeDtypeStruct((feats, 128), F32)...  203 us

profile of v2, /device:TPU:0, one launch (start us, length us, event | category | flops | bytes accessed | tf_op | source)
XLA Modules:
  0.0 207.0 jit_solution(8331799134034592427)
XLA Ops:
  0.6 203.0 %subspace.1 = (f32[2048,128]{1,0:T(8,128)}, f32[1,128]{1,0:T(1,128)}) custom-call(bf16[8192,2048]{1,0:T(8,128)(2,1)} %a_hbm.1, f32[2048,128]{1,0:T(8,128)} %x0_hbm.1), custom_call_target="tpu_custom_call" | custom-call | tf_op jit(solution)/shard_map/subspace/pallas_call | solution.py:314
  203.6 2.3 %copy.6 = f32[2048,128]{1,0:T(8,128)} copy(f32[2048,128]{1,0:T(8,128)} %get-tuple-element.8) | data formatting | bytes 2097152
  205.9 1.1 copy.7
